TPU v7x, 128 devices: a whole 4x4x4 slice. The times are simulated.
128 devices in a mesh: row: 8 (over z, core), col: 16 (over y, x).
Axes of the slice: x: 4, y: 4, z: 4, core: 2. Of those that a mesh axis runs over, the one named last changes fastest.
Arguments:
- coefs: float32 [2, 1536, 16384], P(None, 'row', 'col'), may hold values from -600 to 600, as said below
- tilts: int32 [1536, 2], replicated, may hold values from 8 to 48
- start_basis: float32 [1536, 32], P('col'), may hold values from -6 to 6
Outputs:
- ccc: float32 [1536, 1536], P('row', 'col')
- basis: float32 [1536, 32], P('col')
Inputs may be any that keep to these rules, and one draw needn't show every extreme that they name: `coefs`: real and imaginary parts are products of a particle scale, a coefficient scale and a bounded random value.
All inputs are finite; a program needn't handle non-finite values.
Results may differ from a plain program's by a relative error of at most 0.0003.
Values sent between devices are 32-bit elements; how exact they have to be, the bound alone decides.
No kernel may reach another device: no remote copies, remote signals or barrier semaphores. Data moves between devices by JAX's collectives and lax.ppermute only.
A program may use at most 192 MiB of HBM per device.

v0:
```python
import math

import jax
import jax.numpy as jnp
from jax import lax
from jax.sharding import PartitionSpec as P

GRID = 32
ITERS = 4


EPS = 1e-06
HIGH = lax.Precision.HIGHEST


def in_blocks(array, dim, devices):
    before, after = (array.shape[:dim], array.shape[dim + 1 :])
    return jnp.moveaxis(array.reshape(*before, devices, -1, *after), dim, 0)


def sum_at_owner(array, axis, dim):
    tiles = in_blocks(array, dim, lax.axis_size(axis))
    arrived = lax.all_to_all(tiles, axis, split_axis=0, concat_axis=0, tiled=True)
    return arrived.sum(axis=0)


def from_everyone(array, axis):
    copies = jnp.broadcast_to(array, (lax.axis_size(axis), *array.shape))
    return lax.all_to_all(copies, axis, split_axis=0, concat_axis=0, tiled=True)


def over_copies(array, axis):
    return from_everyone(array, axis).sum(axis=0)


def laid_out(tiles, dim):
    dims = list(tiles.shape[1:])
    dims[dim] *= tiles.shape[0]
    return jnp.moveaxis(tiles, 0, dim).reshape(dims)


def gather_directly(array, axis, dim):
    return laid_out(from_everyone(array, axis), dim)


def wedge(tilt_rows, wave_index):
    wave_x = jnp.abs(wave_index // (GRID * (GRID // 2)) - GRID // 2)[None, :]
    wave_z = (wave_index % GRID - GRID // 2)[None, :]
    upward = wave_z * 16 <= tilt_rows[:, 1:2] * wave_x
    downward = -wave_z * 16 <= tilt_rows[:, 0:1] * wave_x
    return jnp.where(wave_z >= 0, upward, downward).astype(jnp.float32)


def inner(left, right):
    return lax.dot_general(
        left, right, (((1,), (1,)), ((), ())), precision=HIGH, preferred_element_type=jnp.float32
    )


def prepare(values, tilt_rows, wave_index):
    masks = wedge(tilt_rows, wave_index)
    paired = jnp.concatenate([values[0] * masks, values[1] * masks], axis=1)
    energy = masks * (values[0] * values[0] + values[1] * values[1])
    return (masks, paired, energy)


def local(coefs, tilts, start_basis):
    row_count = coefs.shape[1]
    slice_width = coefs.shape[2]
    col_count = start_basis.shape[0]
    col_size = lax.axis_size("col")
    total = col_count * col_size
    row_index = lax.axis_index("row")
    col_index = lax.axis_index("col")
    own_tilts = lax.dynamic_slice_in_dim(tilts, row_index * row_count, row_count, 0)
    wave_index = col_index * slice_width + jnp.arange(slice_width, dtype=jnp.int32)
    own_mask, own_pair, own_energy = prepare(coefs, own_tilts, wave_index)
    gathered = lax.all_gather(coefs, "row", axis=1, tiled=True)
    mask_j, pair_j, energy_j = prepare(gathered, tilts, wave_index)
    numer = inner(pair_j, own_pair)
    first = inner(mask_j, own_energy)
    second = inner(energy_j, own_mask)
    summed = sum_at_owner(jnp.concatenate([numer, first, second], axis=1), "col", 0)
    numer = summed[:, :row_count]
    first = summed[:, row_count : 2 * row_count]
    second = summed[:, 2 * row_count :]
    block = (numer / jnp.sqrt(first * second + EPS)).T
    current = start_basis
    for step in range(ITERS):
        partial_value = jnp.dot(block, current, precision=HIGH, preferred_element_type=jnp.float32)
        summed_rows = over_copies(partial_value, "col")
        local_gram = lax.dot_general(
            summed_rows,
            summed_rows,
            (((0,), (0,)), ((), ())),
            precision=HIGH,
            preferred_element_type=jnp.float32,
        )
        gram = over_copies(local_gram, "row")
        factor = jnp.linalg.cholesky(gram)
        fresh = lax.linalg.triangular_solve(
            factor, summed_rows, left_side=False, lower=True, transpose_a=True
        )
        whole = gather_directly(fresh, "row", 0)
        current = lax.dynamic_slice_in_dim(whole, col_index * col_count, col_count, 0)
    return (block, current * math.sqrt(total))


def solution(mesh):
    in_specs = (P(None, "row", "col"), P(), P("col", None))
    out_specs = (P("row", "col"), P("col", None))
    return jax.shard_map(local, mesh=mesh, in_specs=in_specs, out_specs=out_specs, check_vma=False)
```

profile of v0, /device:TPU:1, one launch (start us, length us, event | category | flops | bytes accessed | tf_op | source)
XLA Modules:
  0.0 345.3 jit_solution(13841363534144779767)
XLA Ops:
  12.5 7.3 %fusion.18 = f32[1536,192]{0,1:T(8,128)} fusion(f32[2,192,1024]{2,1,0:T(8,128)} %param.6, s32[192]{0:T(256)S(1)} %bitcast.109, s32[1024]{0:T(1024)S(1)} %get-tuple-element.21, s32[1024]{0:T(1024)S(1)} %get-tuple-element.20, s32[192]{0:T(256)S(1)} %bitcast.106, s32[1024]{0:T(1024)S(1)} %broadcast_multiply_fusion, ...), kind=kOutput, calls=%fused_computation.29 | convolution fusion | flops 3633512448 | bytes 2797568 | tf_op jit(solution)/shard_map/dot_general | solution.py:55
  19.8 61.0 %all-gather.2.cloned.1.call-done = f32[2,1536,1024]{2,1,0:T(8,128)} async-done(((f32[2,192,1024]{2,1,0:T(8,128)}), f32[2,1536,1024]{2,1,0:T(8,128)}) %all-gather.2.cloned.1.call-update) | async-done | bytes 12582928 | tf_op jit(solution)/shard_map/all_gather | solution.py:78
  80.8 7.4 %fusion.10 = (f32[1536,1024]{1,0:T(8,128)S(1)}, f32[1536,1024]{1,0:T(8,128)S(1)}) fusion(f32[2,1536,1024]{2,1,0:T(8,128)} %all-gather.2.cloned.1.call-done, s32[1536]{0:T(1024)S(1)} %get-tuple-element.13, s32[1024]{0:T(1024)S(1)} %get-tuple-element.21, s32[1024]{0:T(1024)S(1)} %get-tuple-element.20, s32[1536]{0:T(1024)S(1)} %get-tuple-element.12, ...), kind=kLoop, calls=%fused_computation.14 | loop fusion | flops 11010048 | bytes 25191424 | tf_op jit(solution)/shard_map/mul | solution.py:62
  88.2 15.6 %fusion = f32[1536,192]{0,1:T(8,128)} fusion(f32[1536,1024]{1,0:T(8,128)S(1)} %get-tuple-element.15, f32[1536,1024]{1,0:T(8,128)S(1)} %get-tuple-element.14, f32[192,1024]{1,0:T(8,128)} %get-tuple-element.17, f32[192,1024]{1,0:T(8,128)} %get-tuple-element.16), kind=kOutput, calls=%fused_computation | convolution fusion | flops 7251296256 | bytes 15335424 | tf_op jit(solution)/shard_map/dot_general | solution.py:55
  103.9 6.2 %fusion.4 = f32[1536,192]{0,1:T(8,128)S(1)} fusion(f32[2,1536,1024]{2,1,0:T(8,128)S(1)} %bitcast.104, s32[192]{0:T(256)S(1)} %bitcast.110, s32[1024]{0:T(1024)S(1)} %get-tuple-element.21, s32[1024]{0:T(1024)S(1)} %get-tuple-element.20, s32[192]{0:T(256)S(1)} %bitcast.107, s32[1024]{0:T(1024)S(1)} %broadcast_multiply_fusion, ...), kind=kOutput, calls=%fused_computation.6 | convolution fusion | flops 3639017472 | bytes 13807616 | tf_op jit(solution)/shard_map/dot_general | solution.py:55
  110.4 3.1 copy.54
  113.5 54.3 %all_to_all.65 = f32[16,96,576]{2,1,0:T(8,128)} all-to-all(f32[16,96,576]{2,1,0:T(8,128)} %bitcast.102), channel_id=1, replica_groups=mesh['row'=8,'col'=16] {'col'}, dimensions={0} | all-to-all | bytes 7077888 | tf_op jit(solution)/shard_map/all_to_all | solution.py:23
  170.5 13.4 %all_to_all.66 = f32[16,192,32]{1,2,0:T(8,128)S(1)} all-to-all(f32[16,192,32]{1,2,0:T(8,128)S(1)} %broadcast_in_dim.59), channel_id=1, replica_groups=mesh['row'=8,'col'=16] {'col'}, dimensions={0} | all-to-all | bytes 786432 | tf_op jit(solution)/shard_map/all_to_all | solution.py:29
  184.3 10.0 %all_to_all.67 = f32[8,1,1024]{2,1,0:T(1,128)S(1)} all-to-all(f32[8,1,1024]{2,1,0:T(1,128)S(1)} %reshape.98), channel_id=1, replica_groups=mesh['row'=8,'col'=16] {'row'}, dimensions={0} | all-to-all | bytes 65536 | tf_op jit(solution)/shard_map/all_to_all | solution.py:29
  195.7 2.9 cholesky.74
  203.3 4.0 %all-to-all-start.3 = ((f32[8,192,32]{1,2,0:T(8,128)}), f32[8,192,32]{1,2,0:T(8,128)S(1)}, u32[]{:S(2)}, u32[]{:S(2)}) async-start(f32[8,192,32]{1,2,0:T(8,128)} %broadcast_in_dim.61), calls=%async_computation.3 | async-start | bytes 524288 | tf_op jit(solution)/shard_map/all_to_all | solution.py:29
  207.4 6.5 %all-to-all-done.3 = f32[8,192,32]{1,2,0:T(8,128)S(1)} async-done(((f32[8,192,32]{1,2,0:T(8,128)}), f32[8,192,32]{1,2,0:T(8,128)S(1)}, u32[]{:S(2)}, u32[]{:S(2)}) %all-to-all-start.3) | async-done | bytes 196640 | tf_op jit(solution)/shard_map/all_to_all | solution.py:29
  214.4 13.0 %all_to_all.68 = f32[16,192,32]{1,2,0:T(8,128)S(1)} all-to-all(f32[16,192,32]{1,2,0:T(8,128)S(1)} %broadcast_in_dim.62), channel_id=1, replica_groups=mesh['row'=8,'col'=16] {'col'}, dimensions={0} | all-to-all | bytes 786432 | tf_op jit(solution)/shard_map/all_to_all | solution.py:29
  227.8 9.2 %all_to_all.69 = f32[8,1,1024]{2,1,0:T(1,128)S(1)} all-to-all(f32[8,1,1024]{2,1,0:T(1,128)S(1)} %reshape.100), channel_id=1, replica_groups=mesh['row'=8,'col'=16] {'row'}, dimensions={0} | all-to-all | bytes 65536 | tf_op jit(solution)/shard_map/all_to_all | solution.py:29
  238.0 2.9 cholesky.85
  244.9 9.6 %all_to_all.70 = f32[8,192,32]{1,2,0:T(8,128)S(1)} all-to-all(f32[8,192,32]{1,2,0:T(8,128)S(1)} %broadcast_in_dim.64), channel_id=1, replica_groups=mesh['row'=8,'col'=16] {'row'}, dimensions={0} | all-to-all | bytes 393216 | tf_op jit(solution)/shard_map/all_to_all | solution.py:29
  255.1 13.0 %all_to_all.71 = f32[16,192,32]{1,2,0:T(8,128)S(1)} all-to-all(f32[16,192,32]{1,2,0:T(8,128)S(1)} %broadcast_in_dim.65), channel_id=1, replica_groups=mesh['row'=8,'col'=16] {'col'}, dimensions={0} | all-to-all | bytes 786432 | tf_op jit(solution)/shard_map/all_to_all | solution.py:29
  268.5 9.2 %all_to_all.72 = f32[8,1,1024]{2,1,0:T(1,128)S(1)} all-to-all(f32[8,1,1024]{2,1,0:T(1,128)S(1)} %reshape.102), channel_id=1, replica_groups=mesh['row'=8,'col'=16] {'row'}, dimensions={0} | all-to-all | bytes 65536 | tf_op jit(solution)/shard_map/all_to_all | solution.py:29
  278.6 2.9 cholesky.96
  285.6 9.6 %all_to_all.73 = f32[8,192,32]{1,2,0:T(8,128)S(1)} all-to-all(f32[8,192,32]{1,2,0:T(8,128)S(1)} %broadcast_in_dim.67), channel_id=1, replica_groups=mesh['row'=8,'col'=16] {'row'}, dimensions={0} | all-to-all | bytes 393216 | tf_op jit(solution)/shard_map/all_to_all | solution.py:29
  295.8 13.0 %all_to_all.74 = f32[16,192,32]{1,2,0:T(8,128)S(1)} all-to-all(f32[16,192,32]{1,2,0:T(8,128)S(1)} %broadcast_in_dim.68), channel_id=1, replica_groups=mesh['row'=8,'col'=16] {'col'}, dimensions={0} | all-to-all | bytes 786432 | tf_op jit(solution)/shard_map/all_to_all | solution.py:29
  309.2 9.2 %all_to_all.75 = f32[8,1,1024]{2,1,0:T(1,128)S(1)} all-to-all(f32[8,1,1024]{2,1,0:T(1,128)S(1)} %reshape.104), channel_id=1, replica_groups=mesh['row'=8,'col'=16] {'row'}, dimensions={0} | all-to-all | bytes 65536 | tf_op jit(solution)/shard_map/all_to_all | solution.py:29
  327.0 4.0 %all-to-all-start.12 = ((f32[8,192,32]{1,2,0:T(8,128)}), f32[8,192,32]{1,2,0:T(8,128)S(1)}, u32[]{:S(2)}, u32[]{:S(2)}) async-start(f32[8,192,32]{1,2,0:T(8,128)} %broadcast_in_dim.70), calls=%async_computation.12 | async-start | bytes 524288 | tf_op jit(solution)/shard_map/all_to_all | solution.py:29
  331.9 5.6 %all-to-all-done.12 = f32[8,192,32]{1,2,0:T(8,128)S(1)} async-done(((f32[8,192,32]{1,2,0:T(8,128)}), f32[8,192,32]{1,2,0:T(8,128)S(1)}, u32[]{:S(2)}, u32[]{:S(2)}) %all-to-all-start.12) | async-done | bytes 196640 | tf_op jit(solution)/shard_map/all_to_all | solution.py:29
  (105 shorter events, 37.5 us)
Async XLA Ops:
  7.2 163.1 %copy-start = (f32[96,32]{0,1:T(8,128)S(1)}, f32[96,32]{0,1:T(8,128)}, u32[]{:S(2)}) copy-start(f32[96,32]{0,1:T(8,128)} %param.8) | copy-start | bytes 36868
  7.2 73.6 %all-gather.2.cloned.1.call-start = ((), (), s32[]{:S(2)}) async-start(), calls=%async_computation.13 | async-start | bytes 14155776 | tf_op jit(solution)/shard_map/all_gather | solution.py:78
  80.8 23.1 %slice-start = ((s8[12582912]{0:T(1024)(128)(4,1)}), s8[4194304]{0:T(1024)(128)(4,1)S(1)}, s32[]{:S(2)}) async-start(s8[12582912]{0:T(1024)(128)(4,1)} %bitcast.103), calls=%async_computation.14 | async-start | bytes 8388608
  80.8 23.1 %slice-start.1 = ((s8[12582912]{0:T(1024)(128)(4,1)}), s8[4194304]{0:T(1024)(128)(4,1)S(1)}, s32[]{:S(2)}) async-start(s8[12582912]{0:T(1024)(128)(4,1)} %bitcast.103), calls=%async_computation.15 | async-start | bytes 8388608
  88.2 15.7 %slice-start.2 = ((s8[12582912]{0:T(1024)(128)(4,1)}), s8[4194304]{0:T(1024)(128)(4,1)S(1)}, s32[]{:S(2)}) async-start(s8[12582912]{0:T(1024)(128)(4,1)} %bitcast.103), calls=%async_computation.16 | async-start | bytes 8388608
  103.9 6.2 %copy-start.1 = (f32[1536,192]{0,1:T(8,128)S(1)}, f32[1536,192]{0,1:T(8,128)}, u32[]{:S(2)}) copy-start(f32[1536,192]{0,1:T(8,128)} %fusion) | copy-start | bytes 3538948
  103.9 6.2 %copy-start.2 = (f32[1536,192]{0,1:T(8,128)S(1)}, f32[1536,192]{0,1:T(8,128)}, u32[]{:S(2)}) copy-start(f32[1536,192]{0,1:T(8,128)} %fusion.18) | copy-start | bytes 3538948
  203.3 10.5 %all-to-all-start.3 = ((f32[8,192,32]{1,2,0:T(8,128)}), f32[8,192,32]{1,2,0:T(8,128)S(1)}, u32[]{:S(2)}, u32[]{:S(2)}) async-start(f32[8,192,32]{1,2,0:T(8,128)} %broadcast_in_dim.61), calls=%async_computation.3 | async-start | bytes 524288 | tf_op jit(solution)/shard_map/all_to_all | solution.py:29
  327.0 10.5 %all-to-all-start.12 = ((f32[8,192,32]{1,2,0:T(8,128)}), f32[8,192,32]{1,2,0:T(8,128)S(1)}, u32[]{:S(2)}, u32[]{:S(2)}) async-start(f32[8,192,32]{1,2,0:T(8,128)} %broadcast_in_dim.70), calls=%async_computation.12 | async-start | bytes 524288 | tf_op jit(solution)/shard_map/all_to_all | solution.py:29
Sparse Core Ops, SparseCore 0:
  9.7 71.0 all-gather.1
where the time goes:
time: 346 us; the launch traced here: 345 us
  blocking collectives  164 us (47%)
  waiting for transfers between devices  73.8 us (21%)
  other arithmetic  43.6 us (13%)
  matrix products  31.7 us (9%)
  between operations  14.5 us (4%)
  local copies, waits for them, and re-layouts  9.96 us (3%)
  starting transfers between devices  8.13 us (2%)
    all_to_all x10, blocking collectives, from_everyone(): return lax.all_to_all(copies, axis, split_axis=0, concat_axis=0, tiled=True)  109 us
    all_gather x1, waiting for transfers between devices, local(): gathered = lax.all_gather(coefs, 'row', axis=1, tiled=True)  61 us
    all_to_all x1, blocking collectives, sum_at_owner(): lax.all_to_all(tiles, axis, split_axis=0, concat_axis=0, tiled=True)  54.3 us
    dot_general x3, matrix products, inner(): lax.dot_general(left, right, (((1,), (1,)), ((), ())), precision=HIGH, pr...  29.2 us
    another operation x12, other arithmetic, local(): factor = jnp.linalg.cholesky(gram)  14.4 us
    another operation x8, other arithmetic, local(): lax.linalg.triangular_solve(factor, summed_rows, left_side=False, lower=T...  12.3 us
    all_to_all x2, waiting for transfers between devices, from_everyone(): return lax.all_to_all(copies, axis, split_axis=0, concat_axis=0, tiled=True)  12.1 us
    mul x2, other arithmetic, prepare(): paired = jnp.concatenate([values[0] * masks, values[1] * masks], axis=1)  10.3 us
  transfers between devices with their start and end apart: 3, of which 3 were waited for; matrix products, arithmetic and copies ran while one was open for 4% of the time, Pallas kernels for 0%

commit v1 on v0

v1 whole, which is shorter than its diff:
```python
import functools
import math

import jax
import jax.numpy as jnp
from jax import lax
from jax.experimental import pallas as pl
from jax.experimental.pallas import tpu as pltpu
from jax.sharding import PartitionSpec as P

GRID = 32
ITERS = 4
EPS = 1e-06
TILE = 128
SLOTS = 128
VMEM_LIMIT = 24 * 1024 * 1024
HIGH = lax.Precision.HIGHEST


def dot(left, right, contract, precision=None):
    dims = (((contract[0],), (contract[1],)), ((), ()))
    return lax.dot_general(left, right, dims, precision=precision, preferred_element_type=jnp.float32)


def halves(array):
    high = array.astype(jnp.bfloat16)
    return high, (array - high.astype(jnp.float32)).astype(jnp.bfloat16)


def product(left, right, contract):
    total = dot(left[0], right[1], contract) + dot(left[1], right[0], contract)
    return total + dot(left[0], right[0], contract)


def waves(index):
    wave_x = jnp.abs(lax.shift_right_arithmetic(index, 9) - GRID // 2)
    wave_z = jnp.bitwise_and(index, GRID - 1) - GRID // 2
    return wave_x.astype(jnp.float32), wave_z.astype(jnp.float32)


def pairs(blocks):
    return [(a, b) for a in range(blocks) for b in range(a, blocks)]


def sums_kernel(base_ref, mine_ref, theirs_ref, tilts_ref, out_ref, high_ref, low_ref):
    parts, _, rows, depth = mine_ref.shape
    half = parts * rows
    blocks = half // TILE
    tiles = len(pairs(blocks))
    base = base_ref[0]
    wave_x, wave_z = waves(base + lax.broadcasted_iota(jnp.int32, (1, depth), 1))
    upper = wave_z >= 0
    need = 16 * jnp.abs(wave_z)
    row_x, row_z = waves(base + lax.broadcasted_iota(jnp.int32, (depth, SLOTS), 0))
    slot = lax.broadcasted_iota(jnp.int32, (depth, SLOTS), 1)
    reach = jnp.where(slot < 64, slot, slot - 64).astype(jnp.float32) * row_x
    table = (16 * jnp.abs(row_z) <= reach) & ((row_z >= 0) == (slot < 64))
    table = jnp.where(table, 1.0, 0.0).astype(jnp.bfloat16)

    for side, ref in enumerate((mine_ref, theirs_ref)):

        def fill(part, _, side=side, ref=ref):
            start = pl.multiple_of(side * half + part * rows, 64)
            tilt = tilts_ref[pl.ds(start, rows), :]
            limit = jnp.where(upper, tilt[:, 1:2], tilt[:, 0:1]) * wave_x
            keep = need <= limit
            energy = None
            for comp in range(2):
                value = jnp.where(keep, ref[part, comp], 0.0)
                high, low = halves(value)
                high_ref[pl.ds(start, rows), comp * depth : (comp + 1) * depth] = high
                low_ref[pl.ds(start, rows), comp * depth : (comp + 1) * depth] = low
                square = value * value
                energy = square if energy is None else energy + square
            if side == 0:
                high, low = halves(energy)
                spread = dot(high, table, (1, 0)) + dot(low, table, (1, 0))
                out_ref[pl.ds(pl.multiple_of(2 * tiles * TILE + start, 64), rows), :] = spread
            return 0

        lax.fori_loop(0, parts, fill, 0)

    where = {pair: k for k, pair in enumerate(pairs(blocks))}
    wide = 2 * TILE
    for side in range(2):
        for a, b in pairs(half // wide):
            left = slice(a * wide, (a + 1) * wide)
            right = slice(side * half + b * wide, side * half + (b + 1) * wide)
            numer = product(
                (high_ref[left, :], low_ref[left, :]), (high_ref[right, :], low_ref[right, :]), (1, 1)
            )
            for i in range(2):
                for j in range(2):
                    if (2 * a + i, 2 * b + j) in where:
                        k = side * tiles + where[2 * a + i, 2 * b + j]
                        out_ref[k * TILE : (k + 1) * TILE, :] = numer[
                            i * TILE : (i + 1) * TILE, j * TILE : (j + 1) * TILE
                        ]


def matrix_kernel(where_ref, all_ref, partner_ref, tilts_ref, start_ref, high_ref, low_ref, block_ref, wide_ref, spread_ref, hot_ref):
    half, total = high_ref.shape
    blocks = half // TILE
    tri = pairs(blocks)
    tiles = len(tri)
    index = {pair: k for k, pair in enumerate(tri)}
    slot = lax.broadcasted_iota(jnp.int32, (total, SLOTS), 1).astype(jnp.float32)
    hot = (slot == tilts_ref[:, 1:2]) | (slot == tilts_ref[:, 0:1] + 64)
    hot = jnp.where(hot, 1.0, 0.0).astype(jnp.bfloat16)
    hot_ref[:, :SLOTS] = hot
    hot_ref[:, SLOTS:] = hot

    def mine(k):
        per = (all_ref.shape[2] - start_rows) // TILE
        piece, rest = divmod(k, per)
        return all_ref[piece // all_ref.shape[1], piece % all_ref.shape[1], rest * TILE : (rest + 1) * TILE, :]

    start_rows = all_ref.shape[2] % TILE
    for b in range(2 * blocks):
        value = mine(2 * tiles + b) if b < blocks else partner_ref[(tiles + b - blocks) * TILE : (tiles + b - blocks + 1) * TILE, :]
        high, low = halves(value)
        spread_ref[b * TILE : (b + 1) * TILE, :SLOTS] = high
        spread_ref[b * TILE : (b + 1) * TILE, SLOTS:] = low
    for a in range(blocks):
        rows = slice(a * TILE, (a + 1) * TILE)
        scale = dot(spread_ref[rows, :], hot_ref[...], (1, 1)) * dot(hot_ref[rows, :], spread_ref[...], (1, 1)) + EPS
        guess = lax.rsqrt(scale)
        guess = guess * (1.5 - 0.5 * (scale * guess) * guess)
        for b in range(2 * blocks):
            if b < blocks:
                numer = mine(index[a, b]) if a <= b else mine(index[b, a]).T
            elif a <= b - blocks:
                numer = mine(tiles + index[a, b - blocks])
            else:
                k = index[b - blocks, a]
                numer = partner_ref[k * TILE : (k + 1) * TILE, :].T
            cols = slice(b * TILE, (b + 1) * TILE)
            high, low = halves(numer * guess[:, cols])
            high_ref[rows, cols] = high
            low_ref[rows, cols] = low
    n_rows, n_cols = block_ref.shape
    first = pl.multiple_of(where_ref[0], 64)
    pick = lax.broadcasted_iota(jnp.int32, (total, TILE), 0) == (
        lax.broadcasted_iota(jnp.int32, (total, TILE), 1) + where_ref[1]
    )
    pick = jnp.where(pick, 1.0, 0.0).astype(jnp.bfloat16)
    picked = dot(high_ref[pl.ds(first, n_rows), :], pick, (1, 0)) + dot(low_ref[pl.ds(first, n_rows), :], pick, (1, 0))
    block_ref[...] = picked[:, :n_cols]
    wide_ref[...] = product((high_ref[...], low_ref[...]), halves(start_ref[...]), (1, 0))


def inverse_factor(gram):
    size = gram.shape[0]
    columns = [jnp.broadcast_to(gram[j // 8 * 8 :, j : j + 1], (size - j // 8 * 8, TILE)) for j in range(size)]
    inverse = jnp.where(
        lax.broadcasted_iota(jnp.int32, (size, TILE), 0) == lax.broadcasted_iota(jnp.int32, (size, TILE), 1), 1.0, 0.0
    )
    rows = lax.broadcasted_iota(jnp.int32, (size, TILE), 0)
    for k in range(size):
        base = k // 8 * 8
        pivot = jnp.broadcast_to(columns[k][k - base : k - base + 1, :], (8, TILE))
        root = lax.rsqrt(pivot)
        root = root * (1.5 - 0.5 * (pivot * root) * root)
        scaled = columns[k] * jnp.broadcast_to(root[:1], columns[k].shape)
        line = inverse[k : k + 1, :] * root[:1]
        below = jnp.where(rows[base:] > k, scaled, 0.0)
        tail = inverse[base:] - below * line
        tail = jnp.where(rows[base:] == k, line, tail)
        inverse = jnp.concatenate([inverse[:base], tail], axis=0) if base else tail
        for j in range(k + 1, size):
            shift = j // 8 * 8 - base
            columns[j] = columns[j] - scaled[shift:] * scaled[j - base : j - base + 1, :]
    return inverse[:, :size]


def normalized(own_ref, other_ref):
    own, other = own_ref[...], other_ref[...]
    gram = dot(own, own, (0, 0), HIGH) + dot(other, other, (0, 0), HIGH)
    inverse = inverse_factor(gram)
    return dot(own, inverse, (1, 1), HIGH), dot(other, inverse, (1, 1), HIGH)


def step_kernel(high_ref, low_ref, own_ref, other_ref, wide_ref):
    half = own_ref.shape[0]
    own, other = normalized(own_ref, other_ref)
    total = 0.0
    for part, cols in ((own, slice(0, half)), (other, slice(half, 2 * half))):
        total = total + product((high_ref[:, cols], low_ref[:, cols]), halves(part), (1, 0))
    wide_ref[...] = total


def last_kernel(own_ref, other_ref, out_ref):
    half = own_ref.shape[0]
    own, other = normalized(own_ref, other_ref)
    scale = math.sqrt(2 * half)
    out_ref[:half, :] = own * scale
    out_ref[half:, :] = other * scale


def call(body, name, out, inputs, scratch=(), flops=10**9, smem=0):
    vmem = pl.BlockSpec(memory_space=pltpu.VMEM)
    specs = [pl.BlockSpec(memory_space=pltpu.SMEM)] * smem + [vmem] * (len(inputs) - smem)
    return pl.pallas_call(
        body,
        name=name,
        out_shape=out,
        in_specs=specs,
        out_specs=jax.tree.map(lambda _: vmem, out),
        scratch_shapes=list(scratch),
        compiler_params=pltpu.CompilerParams(vmem_limit_bytes=VMEM_LIMIT),
        cost_estimate=pl.CostEstimate(flops=flops, bytes_accessed=10**7, transcendentals=0),
    )(*inputs)


def local(coefs, tilts, start_basis, n_z, n_y, n_x):
    _, rows, width = coefs.shape
    cols, eig = start_basis.shape
    n_row, n_col = 2 * n_z, n_y * n_x
    total = rows * n_row
    half = total // 2
    depth = width // n_z
    blocks = half // TILE
    tiles = len(pairs(blocks))
    f32 = functools.partial(jax.ShapeDtypeStruct, dtype=jnp.float32)
    bf16 = functools.partial(jax.ShapeDtypeStruct, dtype=jnp.bfloat16)
    row = lax.axis_index("row")
    col = lax.axis_index("col")
    z = row // 2
    core = row % 2

    def device(a, c, y, x):
        return (2 * a + c) * n_col + y * n_x + x

    along_x = [[[device(a, c, y, x) for x in range(n_x)] for a in range(n_z) for y in range(n_y)] for c in range(2)]
    along_y = [[[device(a, c, y, x) for y in range(n_y)] for a in range(n_z) for x in range(n_x)] for c in range(2)]
    first_groups = along_x[0] + along_y[1]
    second_groups = along_y[0] + along_x[1]
    z_groups = [[2 * a + c for a in range(n_z)] for c in range(2)]
    swap = [(a, a ^ 1) for a in range(n_row)]

    def over_z(array):
        return lax.all_to_all(array, "row", split_axis=0, concat_axis=0, tiled=True, axis_index_groups=z_groups)

    def over(array, groups):
        return lax.all_to_all(
            array, ("row", "col"), split_axis=0, concat_axis=0, tiled=True, axis_index_groups=groups
        )

    def other_core(array):
        return lax.ppermute(array, "row", swap)

    def to_local(array):
        cut = array.reshape(n_z, 2, rows, -1)
        own = lax.dynamic_index_in_dim(cut, core, 1, keepdims=False).reshape(half, -1)
        other = lax.dynamic_index_in_dim(cut, 1 - core, 1, keepdims=False).reshape(half, -1)
        return jnp.concatenate([own, other], axis=0)

    cut = coefs.reshape(2, rows, n_z, depth).transpose(2, 0, 1, 3)
    mine = over_z(cut)
    theirs = other_core(mine)
    tilts_here = to_local(tilts).astype(jnp.float32)
    base = (col * width + z * depth)[None]
    count = 2 * tiles + blocks
    sums = call(
        sums_kernel,
        "sums",
        f32((count * TILE, TILE)),
        (base, mine, theirs, tilts_here),
        (pltpu.VMEM((total, 2 * depth), jnp.bfloat16), pltpu.VMEM((total, 2 * depth), jnp.bfloat16)),
        smem=1,
    )
    sums = over(sums.reshape(n_x, -1, TILE), first_groups).sum(axis=0)
    sums = over(sums.reshape(n_y, -1, TILE), second_groups).sum(axis=0)
    sums = over_z(jnp.broadcast_to(sums, (n_z, *sums.shape))).sum(axis=0)
    packed = jnp.concatenate([sums, start_basis.reshape(-1, TILE)], axis=0)
    line = over(jnp.broadcast_to(packed, (n_y, *packed.shape)), second_groups)
    everyone = over(jnp.broadcast_to(line, (n_x, *line.shape)), first_groups)
    per = sums.shape[0]
    starts = everyone[:, :, per:]
    starts = jnp.where(core == 0, starts.swapaxes(0, 1), starts)
    start = to_local(starts.reshape(total, eig))
    shared = everyone[:, :, :per].reshape(-1, TILE)[tiles * TILE :]
    partner = other_core(shared)
    owner = (col * cols) // rows
    place = jnp.where(owner % 2 == core, 0, half) + (owner // 2) * rows + (col * cols) % rows
    where = jnp.stack([z * rows, place])
    high, low, block, own = call(
        matrix_kernel,
        "matrix",
        (bf16((half, total)), bf16((half, total)), f32((rows, cols)), f32((half, eig))),
        (where, everyone, partner, tilts_here, start),
        (pltpu.VMEM((total, 2 * SLOTS), jnp.bfloat16), pltpu.VMEM((total, 2 * SLOTS), jnp.bfloat16)),
        smem=1,
    )
    other = other_core(own)
    for _ in range(ITERS - 1):
        own = call(step_kernel, "step", f32((half, eig)), (high, low, own, other))
        other = other_core(own)
    basis = call(last_kernel, "last", f32((total, eig)), (own, other))
    basis = lax.dynamic_slice_in_dim(basis, place, cols, 0)
    return (block, basis)


def solution(mesh):
    n_z = mesh.shape["row"] // 2
    side = math.isqrt(mesh.shape["col"])
    in_specs = (P(None, "row", "col"), P(), P("col", None))
    out_specs = (P("row", "col"), P("col", None))
    body = functools.partial(local, n_z=n_z, n_y=side, n_x=side)
    return jax.shard_map(body, mesh=mesh, in_specs=in_specs, out_specs=out_specs, check_vma=False)
```

time: 346 us -> 177 us (0.51)
  blocking collectives: 164 us -> 98.8 us
  waiting for transfers between devices: 73.8 us -> 17.6 us
  other arithmetic: 43.6 us -> 2.31 us
  matrix products: 31.7 us -> 0 us
  Pallas kernels: 0 us -> 28.1 us
  between operations: 14.5 us -> 0.83 us
  local copies, waits for them, and re-layouts: 9.96 us -> 16 us
  starting transfers between devices: 8.13 us -> 12.6 us
    all_to_all x11 -> x5, blocking collectives: 164 us -> 98.8 us  [the longest x4 73.3 us: over(): lax.all_to_all(array, ('row', 'col'), split_axis=0, concat_axis=0, tiled=...]
    all_gather x1 -> x0, waiting for transfers between devices: 61 us -> none  [local(): gathered = lax.all_gather(coefs, 'row', axis=1, tiled=True)]
    dot_general x11 -> x0, matrix products: 30.7 us -> none  [the longest x3 29.2 us: inner(): lax.dot_general(left, right, (((1,), (1,)), ((), ())), precision=HIGH, pr...]
    pallas_call x0 -> x6, Pallas kernels: none -> 28.1 us  [call(): pl.pallas_call(body, name=name, out_shape=out, in_specs=specs, out_specs=...]
    another operation x20 -> x1, other arithmetic: 26.7 us -> 0.07 us  [local(): where = jnp.stack([z * rows, place])]
    mul x4 -> x0, other arithmetic: 11 us -> none  [the longest x2 10.3 us: prepare(): paired = jnp.concatenate([values[0] * masks, values[1] * masks], axis=1)]
    ppermute x0 -> x6, starting transfers between devices: none -> 9.1 us  [other_core(): return lax.ppermute(array, 'row', swap)]
    ppermute x0 -> x6, waiting for transfers between devices: none -> 8.9 us  [other_core(): return lax.ppermute(array, 'row', swap)]
  transfers between devices with their start and end apart: 3 -> 7, of which waited for: 3 -> 6; matrix products, arithmetic and copies ran while one was open for 4% -> 6% of each run, Pallas kernels for 0% -> 0%
where the time goes in v1:
time: 177 us; the launch traced here: 176 us
  blocking collectives  98.8 us (56%)
  Pallas kernels  28.1 us (16%)
  waiting for transfers between devices  17.6 us (10%)
  local copies, waits for them, and re-layouts  16 us (9%)
  starting transfers between devices  12.6 us (7%)
  other arithmetic  2.31 us (1%)
    all_to_all x4, blocking collectives, over(): lax.all_to_all(array, ('row', 'col'), split_axis=0, concat_axis=0, tiled=...  73.3 us
    pallas_call x6, Pallas kernels, call(): pl.pallas_call(body, name=name, out_shape=out, in_specs=specs, out_specs=...  28.1 us
    all_to_all x1, blocking collectives, over_z(): lax.all_to_all(array, 'row', split_axis=0, concat_axis=0, tiled=True, axi...  25.5 us
    ppermute x6, starting transfers between devices, other_core(): return lax.ppermute(array, 'row', swap)  9.1 us
    ppermute x6, waiting for transfers between devices, other_core(): return lax.ppermute(array, 'row', swap)  8.9 us
    all_to_all x1, waiting for transfers between devices, over_z(): lax.all_to_all(array, 'row', split_axis=0, concat_axis=0, tiled=True, axi...  8.67 us
  transfers between devices with their start and end apart: 7, of which 6 were waited for; matrix products, arithmetic and copies ran while one was open for 6% of the time, Pallas kernels for 0%

profile of v1, /device:TPU:1, one launch (start us, length us, event | category | flops | bytes accessed | tf_op | source)
XLA Modules:
  0.0 176.3 jit_solution(18368911219894134356)
XLA Ops:
  0.6 1.5 copy.52
  2.2 25.5 %all_to_all.30.mine_ref = f32[4,2,192,256]{3,2,1,0:T(8,128)S(1)} all-to-all(f32[4,2,192,256]{3,2,1,0:T(8,128)S(1)} %bitcast.27), channel_id=1, replica_groups={{0,32,64,96},{16,48,80,112},{1,33,65,97},{17,49,81,113},{2,34,66,98},{1..., dimensions={0} | all-to-all | bytes 3145728 | tf_op jit(solution)/shard_map/all_to_all | solution.py:242
  27.7 1.8 %collective-permute-start = (f32[4,2,192,256]{3,2,1,0:T(8,128)S(1)}, f32[4,2,192,256]{3,2,1,0:T(8,128)}, u32[]{:S(2)}, u32[]{:S(2)}) collective-permute-start(f32[4,2,192,256]{3,2,1,0:T(8,128)S(1)} %all_to_all.30.mine_ref), channel_id=1, source_target_pairs={{0,16},{16,0},{32,48},{48,32},{64,80},{80,64},{96,112},{112,96},{1... | collective-permute-start | bytes 4718600 | tf_op jit(solution)/shard_map/ppermute | solution.py:250
  30.2 2.4 %collective-permute-done.theirs_ref = f32[4,2,192,256]{3,2,1,0:T(8,128)} collective-permute-done((f32[4,2,192,256]{3,2,1,0:T(8,128)S(1)}, f32[4,2,192,256]{3,2,1,0:T(8,128)}, u32[]{:S(2)}, u32[]{:S(2)}) %collective-permute-start) | collective-permute-done | bytes 1572896 | tf_op jit(solution)/shard_map/ppermute | solution.py:250
  32.7 6.2 %sums.1 = f32[6144,128]{1,0:T(8,128)S(1)} custom-call(s32[1]{0:T(128)} %bitcast.2.base_ref, f32[4,2,192,256]{3,2,1,0:T(8,128)S(1)} %all_to_all.30.mine_ref, f32[4,2,192,256]{3,2,1,0:T(8,128)} %collective-permute-done.theirs_ref, f32[1536,2]{1,0:T(8,128)S(1)} %convert_element_type.3.tilts_ref), custom_call_target="tpu_custom_call" | custom-call | flops 1000000000 | bytes 10000000 | tf_op jit(solution)/shard_map/sums/pallas_call | solution.py:203
  38.9 25.3 %all_to_all.31 = f32[4,1536,128]{2,1,0:T(8,128)S(1)} all-to-all(f32[4,1536,128]{2,1,0:T(8,128)S(1)} %bitcast.25), channel_id=1, replica_groups={{0,1,2,3},{4,5,6,7},{8,9,10,11},{12,13,14,15},{32,33,34,35},{36,37,38,3..., dimensions={0} | all-to-all | bytes 6291456 | tf_op jit(solution)/shard_map/all_to_all | solution.py:245
  65.2 12.2 %all_to_all.32 = f32[4,384,128]{2,1,0:T(8,128)S(1)} all-to-all(f32[4,384,128]{2,1,0:T(8,128)} %bitcast.28), channel_id=1, replica_groups={{0,4,8,12},{1,5,9,13},{2,6,10,14},{3,7,11,15},{32,36,40,44},{33,37,41,4..., dimensions={0} | all-to-all | bytes 1572864 | tf_op jit(solution)/shard_map/all_to_all | solution.py:245
  78.4 3.5 %all-to-all-start.3 = ((f32[4,384,128]{2,1,0:T(8,128)}), f32[4,384,128]{2,1,0:T(8,128)S(1)}, u32[]{:S(2)}, u32[]{:S(2)}) async-start(f32[4,384,128]{2,1,0:T(8,128)} %broadcast_in_dim.13), calls=%async_computation.3 | async-start | bytes 1572864 | tf_op jit(solution)/shard_map/all_to_all | solution.py:242
  82.1 8.7 %all-to-all-done.3 = f32[4,384,128]{2,1,0:T(8,128)S(1)} async-done(((f32[4,384,128]{2,1,0:T(8,128)}), f32[4,384,128]{2,1,0:T(8,128)S(1)}, u32[]{:S(2)}, u32[]{:S(2)}) %all-to-all-start.3) | async-done | bytes 786464 | tf_op jit(solution)/shard_map/all_to_all | solution.py:242
  90.9 11.0 %all_to_all.33 = f32[4,408,128]{2,1,0:T(8,128)S(1)} all-to-all(f32[4,408,128]{2,1,0:T(8,128)S(1)} %broadcast_in_dim.14), channel_id=1, replica_groups={{0,4,8,12},{1,5,9,13},{2,6,10,14},{3,7,11,15},{32,36,40,44},{33,37,41,4..., dimensions={0} | all-to-all | bytes 1671168 | tf_op jit(solution)/shard_map/all_to_all | solution.py:245
  102.1 24.8 %all_to_all.34.all_ref = f32[4,4,408,128]{3,2,1,0:T(8,128)S(1)} all-to-all(f32[4,4,408,128]{3,2,1,0:T(8,128)S(1)} %broadcast_in_dim.15), channel_id=1, replica_groups={{0,1,2,3},{4,5,6,7},{8,9,10,11},{12,13,14,15},{32,33,34,35},{36,37,38,3..., dimensions={0} | all-to-all | bytes 6684672 | tf_op jit(solution)/shard_map/all_to_all | solution.py:245
  128.6 6.4 %collective-permute-start.1 = (f32[3456,128]{1,0:T(8,128)}, f32[3456,128]{1,0:T(8,128)}, u32[]{:S(2)}, u32[]{:S(2)}) collective-permute-start(f32[3456,128]{1,0:T(8,128)} %slice.13), channel_id=1, source_target_pairs={{0,16},{16,0},{32,48},{48,32},{64,80},{80,64},{96,112},{112,96},{1... | collective-permute-start | bytes 5308424 | tf_op jit(solution)/shard_map/ppermute | solution.py:250
  136.2 2.1 %constant_dynamic-slice_fusion.2 = (f32[4,1,192,32]{3,2,1,0:T(8,128)}, f32[4,1,192,32]{3,2,1,0:T(8,128)}) fusion(f32[4,2,192,32]{3,2,1,0:T(8,128)} %reshape_reshape.3, s32[]{:T(128)S(6)} %select_n.57, s32[]{:T(128)S(6)} %select_n.58), kind=kLoop, calls=%fused_computation.9 | loop fusion | bytes 393224 | tf_op jit(solution)/shard_map/jit(dynamic_index_in_dim)/dynamic_slice | solution.py:254
  138.2 1.8 %copy.45 = f32[768,32]{0,1:T(8,128)} copy(f32[768,32]{1,0:T(8,128)} %bitcast.31) | data formatting | bytes 196608 | tf_op jit(solution)/shard_map/reshape | solution.py:254
  140.0 1.8 %copy.46 = f32[768,32]{0,1:T(8,128)} copy(f32[768,32]{1,0:T(8,128)} %bitcast.30) | data formatting | bytes 196608 | tf_op jit(solution)/shard_map/reshape | solution.py:255
  146.2 8.2 %matrix.1 = (bf16[768,1536]{1,0:T(8,128)(2,1)S(1)}, bf16[768,1536]{1,0:T(8,128)(2,1)S(1)}, f32[192,96]{1,0:T(8,128)}, f32[768,32]{1,0:T(8,128)S(1)}) custom-call(s32[2]{0:T(128)S(1)} %pad_add_fusion.1.where_ref, f32[4,4,408,128]{3,2,1,0:T(8,128)S(1)} %all_to_all.34.all_ref, f32[3456,128]{1,0:T(8,128)} %collective-permute-done.1.partner_ref, ...), custom_call_target="tpu_custom_call" | custom-call | flops 1000000000 | bytes 10000000 | tf_op jit(solution)/shard_map/matrix/pallas_call | solution.py:203
  154.7 1.7 collective-permute-done.2.other_ref
  156.4 3.9 %step.3.own_ref = f32[768,32]{1,0:T(8,128)S(1)} custom-call(bf16[768,1536]{1,0:T(8,128)(2,1)S(1)} %get-tuple-element.7.high_ref, bf16[768,1536]{1,0:T(8,128)(2,1)S(1)} %get-tuple-element.8.low_ref, f32[768,32]{1,0:T(8,128)S(1)} %get-tuple-element.9.own_ref, f32[768,32]{1,0:T(8,128)S(1)} %collective-permute-done.2.other_ref), custom_call_target="tpu_custom_call" | custom-call | flops 1000000000 | bytes 10000000 | tf_op jit(solution)/shard_map/step/pallas_call | solution.py:203
  160.5 1.6 collective-permute-done.3.other_ref
  162.1 3.9 %step.4.own_ref = f32[768,32]{1,0:T(8,128)S(1)} custom-call(bf16[768,1536]{1,0:T(8,128)(2,1)S(1)} %get-tuple-element.7.high_ref, bf16[768,1536]{1,0:T(8,128)(2,1)S(1)} %get-tuple-element.8.low_ref, f32[768,32]{1,0:T(8,128)S(1)} %step.3.own_ref, f32[768,32]{1,0:T(8,128)S(1)} %collective-permute-done.3.other_ref), custom_call_target="tpu_custom_call" | custom-call | flops 1000000000 | bytes 10000000 | tf_op jit(solution)/shard_map/step/pallas_call | solution.py:203
  166.2 1.6 collective-permute-done.4.other_ref
  167.8 3.9 %step.5.own_ref = f32[768,32]{1,0:T(8,128)S(1)} custom-call(bf16[768,1536]{1,0:T(8,128)(2,1)S(1)} %get-tuple-element.7.high_ref, bf16[768,1536]{1,0:T(8,128)(2,1)S(1)} %get-tuple-element.8.low_ref, f32[768,32]{1,0:T(8,128)S(1)} %step.4.own_ref, f32[768,32]{1,0:T(8,128)S(1)} %collective-permute-done.4.other_ref), custom_call_target="tpu_custom_call" | custom-call | flops 1000000000 | bytes 10000000 | tf_op jit(solution)/shard_map/step/pallas_call | solution.py:203
  171.9 1.6 collective-permute-done.5.other_ref
  173.5 2.0 %last.1 = f32[1536,32]{1,0:T(8,128)S(1)} custom-call(f32[768,32]{1,0:T(8,128)S(1)} %step.5.own_ref, f32[768,32]{1,0:T(8,128)S(1)} %collective-permute-done.5.other_ref), custom_call_target="tpu_custom_call" | custom-call | flops 1000000000 | bytes 10000000 | tf_op jit(solution)/shard_map/last/pallas_call | solution.py:203
  (41 shorter events, 12.1 us)
Async XLA Ops:
  2.2 27.3 %copy-start.4 = (s32[1536,2]{0,1:T(2,128)S(1)}, s32[1536,2]{0,1:T(2,128)}, u32[]{:S(2)}) copy-start(s32[1536,2]{0,1:T(2,128)} %param.4) | copy-start | bytes 36868
  27.7 5.0 %collective-permute-start = (f32[4,2,192,256]{3,2,1,0:T(8,128)S(1)}, f32[4,2,192,256]{3,2,1,0:T(8,128)}, u32[]{:S(2)}, u32[]{:S(2)}) collective-permute-start(f32[4,2,192,256]{3,2,1,0:T(8,128)S(1)} %all_to_all.30.mine_ref), channel_id=1, source_target_pairs={{0,16},{16,0},{32,48},{48,32},{64,80},{80,64},{96,112},{112,96},{1... | collective-permute-start | bytes 4718600 | tf_op jit(solution)/shard_map/ppermute | solution.py:250
  30.2 8.6 %copy-start = (f32[1536,2]{1,0:T(8,128)}, f32[1536,2]{1,0:T(8,128)S(1)}, u32[]{:S(2)}) copy-start(f32[1536,2]{1,0:T(8,128)S(1)} %convert_element_type.3.tilts_ref) | copy-start | bytes 36868
  65.2 16.7 %copy-start.3 = (f32[96,32]{0,1:T(8,128)S(1)}, f32[96,32]{0,1:T(8,128)}, u32[]{:S(2)}) copy-start(f32[96,32]{0,1:T(8,128)} %param.5) | copy-start | bytes 36868
  78.4 12.4 %all-to-all-start.3 = ((f32[4,384,128]{2,1,0:T(8,128)}), f32[4,384,128]{2,1,0:T(8,128)S(1)}, u32[]{:S(2)}, u32[]{:S(2)}) async-start(f32[4,384,128]{2,1,0:T(8,128)} %broadcast_in_dim.13), calls=%async_computation.3 | async-start | bytes 1572864 | tf_op jit(solution)/shard_map/all_to_all | solution.py:242
  128.6 15.3 %collective-permute-start.1 = (f32[3456,128]{1,0:T(8,128)}, f32[3456,128]{1,0:T(8,128)}, u32[]{:S(2)}, u32[]{:S(2)}) collective-permute-start(f32[3456,128]{1,0:T(8,128)} %slice.13), channel_id=1, source_target_pairs={{0,16},{16,0},{32,48},{48,32},{64,80},{80,64},{96,112},{112,96},{1... | collective-permute-start | bytes 5308424 | tf_op jit(solution)/shard_map/ppermute | solution.py:250
  143.9 1.1 copy-start.1
  145.0 1.1 copy-start.2
  154.4 2.0 %collective-permute-start.2 = (f32[768,32]{1,0:T(8,128)S(1)}, f32[768,32]{1,0:T(8,128)S(1)}, u32[]{:S(2)}, u32[]{:S(2)}) collective-permute-start(f32[768,32]{1,0:T(8,128)S(1)} %get-tuple-element.9.own_ref), channel_id=1, source_target_pairs={{0,16},{16,0},{32,48},{48,32},{64,80},{80,64},{96,112},{112,96},{1... | collective-permute-start | bytes 294920 | tf_op jit(solution)/shard_map/ppermute | solution.py:250
  160.3 1.8 %collective-permute-start.3 = (f32[768,32]{1,0:T(8,128)S(1)}, f32[768,32]{1,0:T(8,128)S(1)}, u32[]{:S(2)}, u32[]{:S(2)}) collective-permute-start(f32[768,32]{1,0:T(8,128)S(1)} %step.3.own_ref), channel_id=1, source_target_pairs={{0,16},{16,0},{32,48},{48,32},{64,80},{80,64},{96,112},{112,96},{1... | collective-permute-start | bytes 294920 | tf_op jit(solution)/shard_map/ppermute | solution.py:250
  166.0 1.8 %collective-permute-start.4 = (f32[768,32]{1,0:T(8,128)S(1)}, f32[768,32]{1,0:T(8,128)S(1)}, u32[]{:S(2)}, u32[]{:S(2)}) collective-permute-start(f32[768,32]{1,0:T(8,128)S(1)} %step.4.own_ref), channel_id=1, source_target_pairs={{0,16},{16,0},{32,48},{48,32},{64,80},{80,64},{96,112},{112,96},{1... | collective-permute-start | bytes 294920 | tf_op jit(solution)/shard_map/ppermute | solution.py:250
  171.7 1.8 %collective-permute-start.5 = (f32[768,32]{1,0:T(8,128)S(1)}, f32[768,32]{1,0:T(8,128)S(1)}, u32[]{:S(2)}, u32[]{:S(2)}) collective-permute-start(f32[768,32]{1,0:T(8,128)S(1)} %step.5.own_ref), channel_id=1, source_target_pairs={{0,16},{16,0},{32,48},{48,32},{64,80},{80,64},{96,112},{112,96},{1... | collective-permute-start | bytes 294920 | tf_op jit(solution)/shard_map/ppermute | solution.py:250
